TPU v7x, 32 devices: a whole 2x2x4 slice. The times are simulated.
32 devices in a mesh: row: 8 (over z, core), col: 4 (over y, x).
Axes of the slice: x: 2, y: 2, z: 4, core: 2. Of those that a mesh axis runs over, the one named last changes fastest.
Arguments:
- act_codes: int32 [512, 7168], P('col', 'row'), may hold values from -127 to 127
- act_scales: float32 [512, 112], P('col', 'row'), may hold values from 0.005 to 0.03
- gate_weight: bfloat16 [7168, 18432], P('row', 'col'), may hold values from -0.0625 to 0.0625
- up_weight: bfloat16 [7168, 18432], P('row', 'col'), may hold values from -0.0625 to 0.0625
- down_weight: bfloat16 [18432, 7168], P('col', 'row'), may hold values from -0.046875 to 0.046875
Outputs:
- mixed: bfloat16 [512, 7168], P('col', 'row')
All inputs are finite; a program needn't handle non-finite values.
Results may differ from a plain program's by a relative error of at most 0.03.
Values may be sent and summed in bfloat16 or wider, within the bound.
A program may use at most 128 MiB of HBM per device.

v0:
```python
import functools

import jax
import jax.numpy as jnp
from jax import lax
from jax.experimental import pallas as pl
from jax.experimental.pallas import tpu as pltpu
from jax.sharding import PartitionSpec as P

MESH = pl.DeviceIdType.MESH
GROUPS = 2
WIDTHS = (256, 384, 128)
AHEAD = 2
ROWS_PER_DOT = 256
HOP_STEPS = 2


def body(
    n_row, n_col, x_ref, gate_hbm, up_hbm, down_hbm, o_ref,
    every, gate_w, up_w, down_w, part, from_core, from_chip, hid, acc, out_send, out_recv,
    w_sem, act_s, act_r, core_s, core_r, chip_s, chip_r, hz_s, hz_r, hc_s, hc_r, out_s, out_r,
):
    groups, _, piece, depth = x_ref.shape
    chunks, _, width = gate_w.shape
    steps = groups * chunks
    n_chip = n_row // 2
    rows = n_col * piece

    row, col = lax.axis_index("row"), lax.axis_index("col")
    chip, core = row // 2, row % 2
    pos = jnp.where(core == 0, chip, n_chip - 1 - chip)
    ahead_row = row + jnp.where(core == 0, 2, -2)
    behind_row = row - jnp.where(core == 0, 2, -2)
    other_row = chip * 2 + 1 - core
    is_first, is_last = pos == 0, pos == n_chip - 1

    def weight_copy(kind, j):
        columns = pl.ds(j * width, width)
        if kind == 0:
            return pltpu.make_async_copy(gate_hbm.at[:, columns], gate_w.at[j], w_sem.at[0, j])
        if kind == 1:
            return pltpu.make_async_copy(up_hbm.at[:, columns], up_w.at[j], w_sem.at[1, j])
        return pltpu.make_async_copy(down_hbm.at[columns, :], down_w.at[j], w_sem.at[2, j])

    for j in range(chunks):
        weight_copy(0, j).start()
        weight_copy(1, j).start()

    barrier = pltpu.get_barrier_semaphore()
    for p in range(1, n_col):
        pl.semaphore_signal(barrier, inc=1, device_id={"col": lax.rem(col + p, n_col)}, device_id_type=MESH)
    pl.semaphore_signal(barrier, inc=1, device_id={"row": other_row}, device_id_type=MESH)

    @pl.when(chip > 0)
    def _():
        pl.semaphore_signal(barrier, inc=1, device_id={"row": row - 2}, device_id_type=MESH)

    @pl.when(chip < n_chip - 1)
    def _():
        pl.semaphore_signal(barrier, inc=1, device_id={"row": row + 2}, device_id_type=MESH)

    neighbours = jnp.where(chip > 0, 1, 0) + jnp.where(chip < n_chip - 1, 1, 0)
    pl.semaphore_wait(barrier, n_col + neighbours)

    def remote(src, dst, send, recv, where):
        return pltpu.make_async_remote_copy(
            src_ref=src, dst_ref=dst, send_sem=send, recv_sem=recv, device_id=where, device_id_type=MESH
        )

    def act_copy(g, p):
        return remote(
            x_ref.at[g], every.at[g, :, col], act_s.at[g, p], act_r.at[g, col], {"col": lax.rem(col + p, n_col)}
        )

    def act_arrival(g, p):
        source = lax.rem(col + p, n_col)
        return remote(x_ref.at[g], every.at[g, :, source], act_s.at[g, p], act_r.at[g, source], {"col": source})

    def core_copy(j):
        return remote(part.at[j, 1 - core], from_core.at[j], core_s.at[j], core_r.at[j], {"row": other_row})

    def chip_copy(j):
        return remote(part.at[j, core], from_chip.at[j], chip_s.at[j], chip_r.at[j], {"row": ahead_row})

    def hidden_back(j):
        return remote(hid.at[j, core], hid.at[j, core], hz_s.at[j], hz_r.at[j], {"row": behind_row})

    def hidden_across(j):
        return remote(hid.at[j, core], hid.at[j, core], hc_s.at[j], hc_r.at[j], {"row": other_row})

    def hidden_crossed(j):
        return remote(hid.at[j, 1 - core], hid.at[j, 1 - core], hc_s.at[j], hc_r.at[j], {"row": other_row})

    def out_copy(g, p):
        peer = lax.rem(col + p, n_col)
        return remote(out_send.at[g, peer], out_recv.at[g, col], out_s.at[g, p], out_r.at[g, col], {"col": peer})

    def out_arrival(g, p):
        source = lax.rem(col + p, n_col)
        return remote(out_send.at[g, source], out_recv.at[g, source], out_s.at[g, p], out_r.at[g, source], {"col": source})

    for g in range(groups):
        for p in range(1, n_col):
            act_copy(g, p).start()
        for side in range(2):
            every[g, side, col] = x_ref[g, side]
    for j in range(chunks):
        weight_copy(2, j).start()
    acc[...] = jnp.zeros_like(acc)

    tile = min(ROWS_PER_DOT, 2 * rows)
    side_tile = min(tile, rows)

    def multiply(j):
        g, jj = j // chunks, lax.rem(j, chunks)

        @pl.when(jj == 0)
        def _():
            for p in range(1, n_col):
                act_arrival(g, p).wait_recv()

        @pl.when(g == 0)
        def _():
            weight_copy(0, jj).wait()
            weight_copy(1, jj).wait()

        taken = tile // piece
        for side_at in range(0, 2 * n_col, taken):
            if taken > n_col:
                x = every[g].reshape(2 * rows, depth)
            else:
                x = every[g, side_at // n_col, side_at % n_col:side_at % n_col + taken].reshape(tile, depth)
            for half, w in enumerate((gate_w, up_w)):
                y = jnp.dot(x, w[jj], preferred_element_type=jnp.float32).astype(jnp.bfloat16)
                lanes = slice(half * width, (half + 1) * width)
                if taken > n_col:
                    part[j, :, :, lanes] = y.reshape(2, rows, width)
                else:
                    first = (side_at % n_col) * piece
                    part[j, side_at // n_col, first:first + tile, lanes] = y
        core_copy(j).start()

    def add_up(j):
        core_copy(j).wait_recv()

        @pl.when(is_first)
        def _():
            for r in range(0, rows, side_tile):
                at = slice(r, r + side_tile)
                part[j, core, at] = (
                    part[j, core, at].astype(jnp.float32) + from_core[j, at].astype(jnp.float32)
                ).astype(jnp.bfloat16)
            chip_copy(j).start()

        @pl.when(jnp.logical_not(is_first))
        def _():
            chip_copy(j).wait_recv()

        @pl.when(jnp.logical_not(is_first) & jnp.logical_not(is_last))
        def _():
            for r in range(0, rows, side_tile):
                at = slice(r, r + side_tile)
                part[j, core, at] = (
                    part[j, core, at].astype(jnp.float32)
                    + from_core[j, at].astype(jnp.float32)
                    + from_chip[j, at].astype(jnp.float32)
                ).astype(jnp.bfloat16)
            chip_copy(j).start()

        @pl.when(is_last)
        def _():
            for r in range(0, rows, side_tile):
                at = slice(r, r + side_tile)

                def total(lanes):
                    return (
                        part[j, core, at, lanes].astype(jnp.float32)
                        + from_core[j, at, lanes].astype(jnp.float32)
                        + from_chip[j, at, lanes].astype(jnp.float32)
                    )

                gate, up = total(slice(0, width)), total(slice(width, 2 * width))
                hid[j, core, at] = (gate / (1.0 + jnp.exp(-gate)) * up).astype(jnp.bfloat16)
            hidden_back(j).start()
            hidden_across(j).start()

    def pass_on(j):
        hidden_back(j).wait_recv()

        @pl.when(jnp.logical_not(is_first))
        def _():
            hidden_back(j).start()

        hidden_across(j).start()

    def multiply_down(j):
        jj = lax.rem(j, chunks)
        hidden_crossed(j).wait_recv()

        @pl.when(j < chunks)
        def _():
            weight_copy(2, jj).wait()

        for r in range(0, 2 * rows, tile):
            if tile > rows:
                h = hid[j].reshape(2 * rows, width)
            else:
                h = hid[j, r // rows, r % rows:r % rows + tile]
            acc[r:r + tile] += jnp.dot(h, down_w[jj], preferred_element_type=jnp.float32)

    def hand_out(g):
        for side in range(2):
            for k in range(n_col):
                first = side * rows + k * piece
                out_send[g, k, side] = acc[first:first + piece].astype(jnp.bfloat16)
        acc[...] = jnp.zeros_like(acc)
        for p in range(1, n_col):
            out_copy(g, p).start()

    lag = jnp.maximum(HOP_STEPS * 2 * (n_chip - 1 - pos), 1)
    down_lag = jnp.maximum(lag, HOP_STEPS * (n_chip - 1) + 1)

    early = AHEAD + HOP_STEPS * jnp.maximum(2 * pos - (n_chip - 1), 0)
    early = jnp.minimum(early, steps)

    def begin(j, carry):
        multiply(j)
        return carry

    lax.fori_loop(0, early, begin, 0)

    def step(i, carry):
        @pl.when(i + early < steps)
        def _():
            multiply(i + early)

        @pl.when(i < steps)
        def _():
            add_up(i)

        @pl.when((i >= lag) & (i - lag < steps) & jnp.logical_not(is_last))
        def _():
            pass_on(i - lag)

        @pl.when(i >= down_lag)
        def _():
            j = i - down_lag
            multiply_down(j)

            @pl.when(lax.rem(j, chunks) == chunks - 1)
            def _():
                hand_out(j // chunks)

        return carry

    lax.fori_loop(0, steps + down_lag, step, 0)

    for g in range(groups):
        for p in range(1, n_col):
            out_arrival(g, p).wait_recv()
        for side in range(2):
            total = out_send[g, col, side].astype(jnp.float32)
            for p in range(1, n_col):
                total += out_recv[g, lax.rem(col + p, n_col), side].astype(jnp.float32)
            o_ref[g, side] = total.astype(o_ref.dtype)

    def drain(j, carry):
        core_copy(j).wait_send()
        hidden_across(j).wait_send()

        @pl.when(jnp.logical_not(is_last))
        def _():
            chip_copy(j).wait_send()

        @pl.when(jnp.logical_not(is_first))
        def _():
            hidden_back(j).wait_send()

        return carry

    lax.fori_loop(0, steps, drain, 0)
    for g in range(groups):
        for p in range(1, n_col):
            act_copy(g, p).wait_send()
            out_copy(g, p).wait_send()


def on_device(n_row, n_col, act_codes, act_scales, gate_weight, up_weight, down_weight):
    tokens, depth = act_codes.shape
    nblocks = act_scales.shape[1]
    hidden, out_width = down_weight.shape
    blocked = act_codes.astype(jnp.float32).reshape(tokens, nblocks, depth // nblocks)
    acts = (blocked * act_scales[:, :, None]).reshape(tokens, depth).astype(jnp.bfloat16)

    groups = GROUPS
    piece = tokens // (2 * groups)
    width = next(w for w in WIDTHS if hidden % w == 0)
    chunks = hidden // width
    steps = groups * chunks
    rows = n_col * piece
    bf16 = jnp.bfloat16
    dma = pltpu.SemaphoreType.DMA
    out = pl.pallas_call(
        functools.partial(body, n_row, n_col),
        out_shape=jax.ShapeDtypeStruct((groups, 2, piece, out_width), bf16),
        in_specs=[pl.BlockSpec(memory_space=pltpu.VMEM)] + [pl.BlockSpec(memory_space=pl.ANY)] * 3,
        out_specs=pl.BlockSpec(memory_space=pltpu.VMEM),
        scratch_shapes=[
            pltpu.VMEM((groups, 2, n_col, piece, depth), bf16),
            pltpu.VMEM((chunks, depth, width), bf16),
            pltpu.VMEM((chunks, depth, width), bf16),
            pltpu.VMEM((chunks, width, out_width), bf16),
            pltpu.VMEM((steps, 2, rows, 2 * width), bf16),
            pltpu.VMEM((steps, rows, 2 * width), bf16),
            pltpu.VMEM((steps, rows, 2 * width), bf16),
            pltpu.VMEM((steps, 2, rows, width), bf16),
            pltpu.VMEM((2 * rows, out_width), jnp.float32),
            pltpu.VMEM((groups, n_col, 2, piece, out_width), bf16),
            pltpu.VMEM((groups, n_col, 2, piece, out_width), bf16),
            dma((3, chunks)),
            dma((groups, n_col)),
            dma((groups, n_col)),
        ]
        + [dma((steps,))] * 8
        + [dma((groups, n_col))] * 2,
        compiler_params=pltpu.CompilerParams(
            collective_id=0, has_side_effects=True, vmem_limit_bytes=67043328
        ),
    )(acts.reshape(groups, 2, piece, depth), gate_weight, up_weight, down_weight)
    return out.reshape(tokens, out_width)


def solution(mesh):
    placed = (P("col", "row"), P("col", "row"), P("row", "col"), P("row", "col"), P("col", "row"))
    return jax.shard_map(
        functools.partial(on_device, mesh.shape["row"], mesh.shape["col"]),
        mesh=mesh,
        in_specs=placed,
        out_specs=P("col", "row"),
        check_vma=False,
    )
```

profile of v0, /device:TPU:0, one launch (start us, length us, event | category | flops | bytes accessed | tf_op | source)
XLA Modules:
  0.0 125.7 jit_solution(14585430256489481666)
XLA Ops:
  0.0 1.2 copy.7
  1.2 0.7 fusion
  2.0 0.8 copy.8
  2.8 121.3 %shard_map.55 = bf16[2,2,32,896]{3,2,1,0:T(8,128)(2,1)} custom-call(bf16[2,2,32,896]{3,2,1,0:T(8,128)(2,1)} %bitcast.6, bf16[896,4608]{1,0:T(8,128)(2,1)} %gate_hbm.1, bf16[896,4608]{1,0:T(8,128)(2,1)} %up_hbm.1, bf16[4608,896]{1,0:T(8,128)(2,1)} %down_hbm.1), custom_call_target="tpu_custom_call" | custom-call | tf_op jit(solution)/shard_map/pallas_call | solution.py:303
  124.1 1.6 %copy.10 = bf16[128,896]{1,0:T(8,128)(2,1)} copy(bf16[128,896]{1,0:T(8,128)(2,1)} %bitcast.7) | data formatting | bytes 458752
where the time goes:
time: 126 us
  Pallas kernels  121 us (96%)
  local copies, waits for them, and re-layouts  3.69 us (3%)
    pallas_call x1, Pallas kernels, on_device(): pl.pallas_call(functools.partial(body, n_row, n_col), out_shape=jax.Shape...  121 us
    unnamed x2, local copies, waits for them, and re-layouts  2.86 us

commit v1 on v0

v1 whole, which is shorter than its diff:
```python
import functools

import jax
import jax.numpy as jnp
from jax import lax
from jax.experimental import pallas as pl
from jax.experimental.pallas import tpu as pltpu
from jax.sharding import PartitionSpec as P

MESH = pl.DeviceIdType.MESH
WIDTHS = (512, 384, 256, 128)
AHEAD = 2
LAG = 28
LAG_HOP = 8
FETCH = 3
EARLY = 2
EARLY_HOP = 3
EARLY_LAST = 3


def body(
    n_row, n_col, codes_hbm, scales_hbm, gate_hbm, up_hbm, down_hbm, o_ref,
    codes, scales, every, up_gate, down_w, part, from_core, from_chip, hid, acc, out_send, out_recv,
    in_sem, w_sem, act_s, act_r, core_s, core_r, chip_s, chip_r, cross_s, cross_r, out_s, out_r,
):
    _, _, half, depth = every.shape
    chunks, _, _, width = up_gate.shape
    steps = n_col * chunks
    n_chip = n_row // 2
    nblocks, tokens = scales.shape
    block = depth // nblocks
    others = (n_col - 1) * chunks
    fetch = min(FETCH, chunks)

    row, col = lax.axis_index("row"), lax.axis_index("col")
    chip, core = row // 2, row % 2
    pos = jnp.where(core == 0, chip, n_chip - 1 - chip)
    ahead_row = row + jnp.where(core == 0, 2, -2)
    behind_row = row - jnp.where(core == 0, 2, -2)
    other_row = chip * 2 + 1 - core
    is_first, is_last = pos == 0, pos == n_chip - 1

    def partner(p):
        there, bit = 0, 1
        while bit < n_col:
            there += bit * lax.rem(col // bit + p // bit, 2)
            bit *= 2
        return there

    def hidden_step(k):
        return jnp.where(k < others, k + chunks, k - others)

    def fetch_up_gate(j):
        columns = pl.ds(j * width, width)
        pltpu.make_async_copy(gate_hbm.at[:, columns], up_gate.at[j, 0], w_sem.at[j]).start()
        pltpu.make_async_copy(up_hbm.at[:, columns], up_gate.at[j, 1], w_sem.at[j]).start()

    def wait_up_gate(j):
        pltpu.make_async_copy(up_gate.at[j], up_gate.at[j], w_sem.at[j]).wait()

    def down_copy(j):
        return pltpu.make_async_copy(down_hbm.at[pl.ds(j * width, width), :], down_w.at[j], w_sem.at[j])

    codes_copy = pltpu.make_async_copy(codes_hbm, codes, in_sem.at[0])
    scales_copy = pltpu.make_async_copy(scales_hbm, scales, in_sem.at[1])
    codes_copy.start()
    scales_copy.start()
    fetch_up_gate(0)

    barrier = pltpu.get_barrier_semaphore()
    for p in range(1, n_col):
        pl.semaphore_signal(barrier, inc=1, device_id={"col": partner(p)}, device_id_type=MESH)
    pl.semaphore_signal(barrier, inc=1, device_id={"row": other_row}, device_id_type=MESH)

    @pl.when(chip > 0)
    def _():
        pl.semaphore_signal(barrier, inc=1, device_id={"row": row - 2}, device_id_type=MESH)

    @pl.when(chip < n_chip - 1)
    def _():
        pl.semaphore_signal(barrier, inc=1, device_id={"row": row + 2}, device_id_type=MESH)

    neighbours = jnp.where(chip > 0, 1, 0) + jnp.where(chip < n_chip - 1, 1, 0)

    def remote(src, dst, send, recv, where):
        return pltpu.make_async_remote_copy(
            src_ref=src, dst_ref=dst, send_sem=send, recv_sem=recv, device_id=where, device_id_type=MESH
        )

    def act_copy(p):
        return remote(every.at[0], every.at[p], act_s, act_r.at[p], {"col": partner(p)})

    def core_copy(j):
        return remote(part.at[j, 1 - core], from_core.at[j], core_s, core_r.at[j], {"row": other_row})

    def chip_copy(j):
        return remote(part.at[j, core], from_chip.at[j], chip_s, chip_r.at[j], {"row": ahead_row})

    def hidden_back(j):
        return remote(hid.at[j, core], hid.at[j, core], chip_s, chip_r.at[j], {"row": behind_row})

    def hidden_across(j):
        return remote(hid.at[j, core], hid.at[j, core], cross_s, cross_r.at[j], {"row": other_row})

    def hidden_crossed(j):
        return remote(hid.at[j, 1 - core], hid.at[j, 1 - core], cross_s, cross_r.at[j], {"row": other_row})

    def out_copy(p):
        return remote(out_send.at[p], out_recv.at[p], out_s, out_r.at[p], {"col": partner(p)})

    def product(j, b, c):
        x = every[b].reshape(2 * half, depth)
        for at in range(2):
            y = jnp.dot(x, up_gate[c, at], preferred_element_type=jnp.float32).astype(jnp.bfloat16)
            part[j, :, :, at * width:(at + 1) * width] = y.reshape(2, half, width)

    codes_copy.wait()
    scales_copy.wait()
    for j in range(1, fetch):
        fetch_up_gate(j)
    by_token = scales[...].T
    for lane in range(0, depth, 128):
        lanes = min(128, depth - lane)
        first = lane // block
        s = by_token[:, first:first + 1]
        at = lax.broadcasted_iota(jnp.int32, (tokens, lanes), 1)
        for k in range(1, lanes // block):
            s = jnp.where(at >= k * block, by_token[:, first + k:first + k + 1], s)
        x = (codes[:, lane:lane + lanes].astype(jnp.float32) * s).astype(jnp.bfloat16)
        every[0, :, :, lane:lane + lanes] = x.reshape(2, half, lanes)
    acc[...] = jnp.zeros_like(acc)

    wait_up_gate(0)
    product(0, 0, 0)

    pl.semaphore_wait(barrier, n_col + neighbours)
    core_copy(0).start()
    for p in range(1, n_col):
        act_copy(p).start()

    def multiply(j):
        b, c = j // chunks, lax.rem(j, chunks)

        @pl.when((b > 0) & (c == 0))
        def _():
            act_copy(b).wait_recv()

        @pl.when(b == 0)
        def _():
            wait_up_gate(c)

            @pl.when(c + fetch - 1 < chunks)
            def _():
                fetch_up_gate(c + fetch - 1)

        @pl.when(b == 1)
        def _():
            down_copy(c).start()

        product(j, b, c)
        core_copy(j).start()

    def add_up(j):
        core_copy(j).wait_recv()

        @pl.when(is_first)
        def _():
            part[j, core] = (
                part[j, core].astype(jnp.float32) + from_core[j].astype(jnp.float32)
            ).astype(jnp.bfloat16)
            chip_copy(j).start()

        @pl.when(jnp.logical_not(is_first))
        def _():
            chip_copy(j).wait_recv()

        @pl.when(jnp.logical_not(is_first) & jnp.logical_not(is_last))
        def _():
            part[j, core] = (
                part[j, core].astype(jnp.float32)
                + from_core[j].astype(jnp.float32)
                + from_chip[j].astype(jnp.float32)
            ).astype(jnp.bfloat16)
            chip_copy(j).start()

        @pl.when(is_last)
        def _():
            def total(lanes):
                return (
                    part[j, core, :, lanes].astype(jnp.float32)
                    + from_core[j, :, lanes].astype(jnp.float32)
                    + from_chip[j, :, lanes].astype(jnp.float32)
                )

            gate, up = total(slice(0, width)), total(slice(width, 2 * width))
            hid[j, core] = (gate / (1.0 + jnp.exp(-gate)) * up).astype(jnp.bfloat16)

    def pass_on(k):
        j = hidden_step(k)

        @pl.when(jnp.logical_not(is_last))
        def _():
            hidden_back(j).wait_recv()

        @pl.when(jnp.logical_not(is_first))
        def _():
            hidden_back(j).start()

        hidden_across(j).start()

    def multiply_down(k):
        j = hidden_step(k)
        c = lax.rem(k, chunks)
        hidden_crossed(j).wait_recv()

        @pl.when(k < chunks)
        def _():
            down_copy(c).wait()

        h = hid[j].reshape(2 * half, width)
        acc[...] += jnp.dot(h, down_w[c], preferred_element_type=jnp.float32)

        @pl.when((k < others) & (c == chunks - 1))
        def _():
            b = k // chunks + 1
            out_send[b] = acc[...].astype(jnp.bfloat16)
            acc[...] = jnp.zeros_like(acc)
            out_copy(b).start()

    lag = LAG + LAG_HOP * (n_chip - 1 - pos)
    down_lag = LAG + LAG_HOP * jnp.maximum(pos, n_chip - 1 - pos) + 2
    early = jnp.minimum(EARLY + EARLY_HOP * pos + jnp.where(is_last, EARLY_LAST, 0), steps)

    def begin(j, carry):
        multiply(j)
        return carry

    lax.fori_loop(1, early, begin, 0)

    def step(i, carry):
        @pl.when(i + early < steps)
        def _():
            multiply(i + early)

        @pl.when(i < steps)
        def _():
            add_up(i)

        @pl.when((i >= lag) & (i - lag < steps))
        def _():
            pass_on(i - lag)

        @pl.when(i >= down_lag)
        def _():
            multiply_down(i - down_lag)

        return carry

    lax.fori_loop(0, steps + down_lag, step, 0)

    total = acc[...]
    for p in range(1, n_col):
        out_copy(p).wait_recv()
        total += out_recv[p].astype(jnp.float32)
    o_ref[...] = total.astype(o_ref.dtype)

    def all_sent(ref, send):
        remote(ref, ref, send, core_r.at[0], {"row": other_row}).wait_send()

    all_sent(from_core, core_s)
    all_sent(hid.at[:, 0], cross_s)

    @pl.when(jnp.logical_not(is_last))
    def _():
        all_sent(from_chip, chip_s)

    @pl.when(jnp.logical_not(is_first))
    def _():
        all_sent(hid.at[:, 0], chip_s)

    all_sent(every.at[pl.ds(1, n_col - 1)], act_s)
    all_sent(out_recv.at[pl.ds(1, n_col - 1)], out_s)


def on_device(n_row, n_col, act_codes, act_scales, gate_weight, up_weight, down_weight):
    tokens, depth = act_codes.shape
    nblocks = act_scales.shape[1]
    hidden, out_width = down_weight.shape
    half = tokens // 2
    width = next(w for w in WIDTHS if hidden % w == 0)
    chunks = hidden // width
    steps = n_col * chunks
    bf16 = jnp.bfloat16
    dma = pltpu.SemaphoreType.DMA
    return pl.pallas_call(
        functools.partial(body, n_row, n_col),
        out_shape=jax.ShapeDtypeStruct((tokens, out_width), bf16),
        in_specs=[pl.BlockSpec(memory_space=pl.ANY)] * 5,
        out_specs=pl.BlockSpec(memory_space=pltpu.VMEM),
        scratch_shapes=[
            pltpu.VMEM((tokens, depth), jnp.int32),
            pltpu.VMEM((nblocks, tokens), jnp.float32),
            pltpu.VMEM((n_col, 2, half, depth), bf16),
            pltpu.VMEM((chunks, 2, depth, width), bf16),
            pltpu.VMEM((chunks, width, out_width), bf16),
            pltpu.VMEM((steps, 2, half, 2 * width), bf16),
            pltpu.VMEM((steps, half, 2 * width), bf16),
            pltpu.VMEM((steps, half, 2 * width), bf16),
            pltpu.VMEM((steps, 2, half, width), bf16),
            pltpu.VMEM((tokens, out_width), jnp.float32),
            pltpu.VMEM((n_col, tokens, out_width), bf16),
            pltpu.VMEM((n_col, tokens, out_width), bf16),
            dma((2,)),
            dma((chunks,)),
            dma,
            dma((n_col,)),
            dma,
            dma((steps,)),
            dma,
            dma((steps,)),
            dma,
            dma((steps,)),
            dma,
            dma((n_col,)),
        ],
        compiler_params=pltpu.CompilerParams(
            collective_id=0, has_side_effects=True, vmem_limit_bytes=67043328
        ),
    )(act_codes, act_scales.T, gate_weight, up_weight, down_weight)


def solution(mesh):
    placed = (P("col", "row"), P("col", "row"), P("row", "col"), P("row", "col"), P("col", "row"))
    return jax.shard_map(
        functools.partial(on_device, mesh.shape["row"], mesh.shape["col"]),
        mesh=mesh,
        in_specs=placed,
        out_specs=P("col", "row"),
        check_vma=False,
    )
```

time: 126 us -> 104 us (0.83)
  Pallas kernels: 121 us -> 102 us
  local copies, waits for them, and re-layouts: 3.69 us -> 1.65 us
    pallas_call x1, Pallas kernels: 121 us -> 102 us  [on_device(): pl.pallas_call(functools.partial(body, n_row, n_col), out_shape=jax.Shape...]
    unnamed x2 -> x1, local copies, waits for them, and re-layouts: 2.86 us -> 1.65 us
where the time goes in v1:
time: 104 us; the launch traced here: 103 us
  Pallas kernels  102 us (98%)
  local copies, waits for them, and re-layouts  1.65 us (2%)
    pallas_call x1, Pallas kernels, on_device(): pl.pallas_call(functools.partial(body, n_row, n_col), out_shape=jax.Shape...  102 us

profile of v1, /device:TPU:0, one launch (start us, length us, event | category | flops | bytes accessed | tf_op | source)
XLA Modules:
  0.0 103.3 jit_solution(237695158447342398)
XLA Ops:
  0.0 101.6 %shard_map.55 = bf16[128,896]{1,0:T(8,128)(2,1)} custom-call(s32[128,896]{1,0:T(8,128)} %codes_hbm.1, f32[14,128]{1,0:T(8,128)} %bitcast.1, bf16[896,4608]{1,0:T(8,128)(2,1)} %gate_hbm.1, bf16[896,4608]{1,0:T(8,128)(2,1)} %up_hbm.1, bf16[4608,896]{1,0:T(8,128)(2,1)} %down_hbm.1), custom_call_target="tpu_custom_call" | custom-call | tf_op jit(solution)/shard_map/pallas_call | solution.py:295
  101.7 1.6 %copy.7 = bf16[128,896]{1,0:T(8,128)(2,1)} copy(bf16[128,896]{1,0:T(8,128)(2,1)} %shard_map.55) | data formatting | bytes 458752

commit v2 on v1

--- a/solution.py
+++ b/solution.py
@@ -10,11 +10,12 @@
 MESH = pl.DeviceIdType.MESH
 WIDTHS = (512, 384, 256, 128)
 AHEAD = 2
-LAG = 28
-LAG_HOP = 8
+BEFORE = (8, 3, 0)
+DOWN_AFTER = 1
+PER_STEP = 2
 FETCH = 3
 EARLY = 2
-EARLY_HOP = 3
+EARLY_HOP = 4
 EARLY_LAST = 3
 
 
@@ -41,6 +42,8 @@
     is_first, is_last = pos == 0, pos == n_chip - 1
 
     def partner(p):
+        middle = n_col // 2
+        p = jnp.where(p < middle, p, jnp.where(p == n_col - 1, middle, p + 1))
         there, bit = 0, 1
         while bit < n_col:
             there += bit * lax.rem(col // bit + p // bit, 2)
@@ -227,8 +230,14 @@
             acc[...] = jnp.zeros_like(acc)
             out_copy(b).start()
 
-    lag = LAG + LAG_HOP * (n_chip - 1 - pos)
-    down_lag = LAG + LAG_HOP * jnp.maximum(pos, n_chip - 1 - pos) + 2
+    def lag_at(place):
+        lag = steps - min(BEFORE[-1], steps // 4)
+        for hops, before in enumerate(BEFORE[:-1]):
+            lag = jnp.where(place == n_chip - 1 - hops, steps - min(before, steps // 4), lag)
+        return lag
+
+    lag = lag_at(pos)
+    down_lag = jnp.maximum(lag, lag_at(n_chip - 1 - pos)) + DOWN_AFTER
     early = jnp.minimum(EARLY + EARLY_HOP * pos + jnp.where(is_last, EARLY_LAST, 0), steps)
 
     def begin(j, carry):
@@ -238,25 +247,30 @@
     lax.fori_loop(1, early, begin, 0)
 
     def step(i, carry):
+        @pl.when(i < steps)
+        def _():
+            add_up(i)
+
         @pl.when(i + early < steps)
         def _():
             multiply(i + early)
 
-        @pl.when(i < steps)
-        def _():
-            add_up(i)
-
-        @pl.when((i >= lag) & (i - lag < steps))
-        def _():
-            pass_on(i - lag)
-
-        @pl.when(i >= down_lag)
-        def _():
-            multiply_down(i - down_lag)
+        for r in range(PER_STEP):
+            k = PER_STEP * (i - lag) + r
+
+            @pl.when((k >= 0) & (k < steps))
+            def _():
+                pass_on(k)
+
+            down = PER_STEP * (i - down_lag) + r
+
+            @pl.when((down >= 0) & (down < steps))
+            def _():
+                multiply_down(down)
 
         return carry
 
-    lax.fori_loop(0, steps + down_lag, step, 0)
+    lax.fori_loop(0, down_lag + pl.cdiv(steps, PER_STEP), step, 0)
 
     total = acc[...]
     for p in range(1, n_col):

time: 104 us -> 99 us (0.952)
  Pallas kernels: 102 us -> 97.1 us
    pallas_call x1, Pallas kernels: 102 us -> 97.1 us  [on_device(): pl.pallas_call(functools.partial(body, n_row, n_col), out_shape=jax.Shape...]
where the time goes in v2:
time: 99 us; the launch traced here: 98.7 us
  Pallas kernels  97.1 us (98%)
  local copies, waits for them, and re-layouts  1.65 us (2%)
    pallas_call x1, Pallas kernels, on_device(): pl.pallas_call(functools.partial(body, n_row, n_col), out_shape=jax.Shape...  97.1 us

profile of v2, /device:TPU:0, one launch (start us, length us, event | category | flops | bytes accessed | tf_op | source)
XLA Modules:
  0.0 98.7 jit_solution(8436224201261477990)
XLA Ops:
  0.0 97.1 %shard_map.55 = bf16[128,896]{1,0:T(8,128)(2,1)} custom-call(s32[128,896]{1,0:T(8,128)} %codes_hbm.1, f32[14,128]{1,0:T(8,128)} %bitcast.1, bf16[896,4608]{1,0:T(8,128)(2,1)} %gate_hbm.1, bf16[896,4608]{1,0:T(8,128)(2,1)} %up_hbm.1, bf16[4608,896]{1,0:T(8,128)(2,1)} %down_hbm.1), custom_call_target="tpu_custom_call" | custom-call | tf_op jit(solution)/shard_map/pallas_call | solution.py:309
  97.1 1.6 %copy.7 = bf16[128,896]{1,0:T(8,128)(2,1)} copy(bf16[128,896]{1,0:T(8,128)(2,1)} %shard_map.55) | data formatting | bytes 458752

commit v3 on v2

--- a/solution.py
+++ b/solution.py
@@ -8,15 +8,17 @@
 from jax.sharding import PartitionSpec as P
 
 MESH = pl.DeviceIdType.MESH
-WIDTHS = (512, 384, 256, 128)
+WIDTHS = (384, 256, 128)
 AHEAD = 2
-BEFORE = (8, 3, 0)
+BEFORE = (9, 4, 1)
 DOWN_AFTER = 1
 PER_STEP = 2
-FETCH = 3
-EARLY = 2
-EARLY_HOP = 4
-EARLY_LAST = 3
+PER_STEP_LAST = 3
+FETCH = 4
+EARLY_FIRST = 2
+EARLY = 4
+EARLY_HOP = 6
+EARLY_LAST = 5
 
 
 def body(
@@ -50,6 +52,9 @@
             bit *= 2
         return there
 
+    def block_at(turn, side):
+        return turn if side == 0 else lax.rem(n_col - turn, n_col)
+
     def hidden_step(k):
         return jnp.where(k < others, k + chunks, k - others)
 
@@ -90,8 +95,9 @@
             src_ref=src, dst_ref=dst, send_sem=send, recv_sem=recv, device_id=where, device_id_type=MESH
         )
 
-    def act_copy(p):
-        return remote(every.at[0], every.at[p], act_s, act_r.at[p], {"col": partner(p)})
+    def act_copy(p, side):
+        at = 2 * p + side
+        return remote(every.at[0, side], every.at[p, side], act_s, act_r.at[at], {"col": partner(p)})
 
     def core_copy(j):
         return remote(part.at[j, 1 - core], from_core.at[j], core_s, core_r.at[j], {"row": other_row})
@@ -108,11 +114,12 @@
     def hidden_crossed(j):
         return remote(hid.at[j, 1 - core], hid.at[j, 1 - core], cross_s, cross_r.at[j], {"row": other_row})
 
-    def out_copy(p):
-        return remote(out_send.at[p], out_recv.at[p], out_s, out_r.at[p], {"col": partner(p)})
-
-    def product(j, b, c):
-        x = every[b].reshape(2 * half, depth)
+    def out_copy(p, side):
+        at = 2 * p + side
+        return remote(out_send.at[p, side], out_recv.at[p, side], out_s, out_r.at[at], {"col": partner(p)})
+
+    def product(j, turn, c):
+        x = jnp.concatenate([every[block_at(turn, side), side] for side in range(2)])
         for at in range(2):
             y = jnp.dot(x, up_gate[c, at], preferred_element_type=jnp.float32).astype(jnp.bfloat16)
             part[j, :, :, at * width:(at + 1) * width] = y.reshape(2, half, width)
@@ -138,17 +145,19 @@
 
     pl.semaphore_wait(barrier, n_col + neighbours)
     core_copy(0).start()
-    for p in range(1, n_col):
-        act_copy(p).start()
+    for turn in range(1, n_col):
+        for side in range(2):
+            act_copy(block_at(turn, side), side).start()
 
     def multiply(j):
-        b, c = j // chunks, lax.rem(j, chunks)
-
-        @pl.when((b > 0) & (c == 0))
-        def _():
-            act_copy(b).wait_recv()
-
-        @pl.when(b == 0)
+        turn, c = j // chunks, lax.rem(j, chunks)
+
+        @pl.when((turn > 0) & (c == 0))
+        def _():
+            for side in range(2):
+                act_copy(block_at(turn, side), side).wait_recv()
+
+        @pl.when(turn == 0)
         def _():
             wait_up_gate(c)
 
@@ -156,11 +165,11 @@
             def _():
                 fetch_up_gate(c + fetch - 1)
 
-        @pl.when(b == 1)
+        @pl.when(turn == 1)
         def _():
             down_copy(c).start()
 
-        product(j, b, c)
+        product(j, turn, c)
         core_copy(j).start()
 
     def add_up(j):
@@ -198,12 +207,14 @@
             gate, up = total(slice(0, width)), total(slice(width, 2 * width))
             hid[j, core] = (gate / (1.0 + jnp.exp(-gate)) * up).astype(jnp.bfloat16)
 
+    def send_back(k):
+        j = hidden_step(k)
+        hidden_back(j).start()
+        hidden_across(j).start()
+
     def pass_on(k):
         j = hidden_step(k)
-
-        @pl.when(jnp.logical_not(is_last))
-        def _():
-            hidden_back(j).wait_recv()
+        hidden_back(j).wait_recv()
 
         @pl.when(jnp.logical_not(is_first))
         def _():
@@ -225,20 +236,23 @@
 
         @pl.when((k < others) & (c == chunks - 1))
         def _():
-            b = k // chunks + 1
-            out_send[b] = acc[...].astype(jnp.bfloat16)
+            for side in range(2):
+                b = block_at(k // chunks + 1, side)
+                out_send[b, side] = acc[side * half:(side + 1) * half].astype(jnp.bfloat16)
+                out_copy(b, side).start()
             acc[...] = jnp.zeros_like(acc)
-            out_copy(b).start()
 
     def lag_at(place):
-        lag = steps - min(BEFORE[-1], steps // 4)
+        most = (steps - chunks) // PER_STEP_LAST
+        lag = steps - min(BEFORE[-1], most)
         for hops, before in enumerate(BEFORE[:-1]):
-            lag = jnp.where(place == n_chip - 1 - hops, steps - min(before, steps // 4), lag)
+            lag = jnp.where(place == n_chip - 1 - hops, steps - min(before, most), lag)
         return lag
 
     lag = lag_at(pos)
     down_lag = jnp.maximum(lag, lag_at(n_chip - 1 - pos)) + DOWN_AFTER
-    early = jnp.minimum(EARLY + EARLY_HOP * pos + jnp.where(is_last, EARLY_LAST, 0), steps)
+    early = EARLY + EARLY_HOP * (pos - 1) + jnp.where(is_last, EARLY_LAST, 0)
+    early = jnp.minimum(jnp.where(is_first, EARLY_FIRST, early), steps)
 
     def begin(j, carry):
         multiply(j)
@@ -255,10 +269,17 @@
         def _():
             multiply(i + early)
 
+        for r in range(PER_STEP_LAST):
+            k = PER_STEP_LAST * (i - lag) + r
+
+            @pl.when((k >= 0) & (k < steps) & is_last)
+            def _():
+                send_back(k)
+
         for r in range(PER_STEP):
             k = PER_STEP * (i - lag) + r
 
-            @pl.when((k >= 0) & (k < steps))
+            @pl.when((k >= 0) & (k < steps) & jnp.logical_not(is_last))
             def _():
                 pass_on(k)
 
@@ -273,9 +294,11 @@
     lax.fori_loop(0, down_lag + pl.cdiv(steps, PER_STEP), step, 0)
 
     total = acc[...]
+    for turn in range(1, n_col):
+        for side in range(2):
+            out_copy(block_at(turn, side), side).wait_recv()
     for p in range(1, n_col):
-        out_copy(p).wait_recv()
-        total += out_recv[p].astype(jnp.float32)
+        total += out_recv[p].reshape(total.shape).astype(jnp.float32)
     o_ref[...] = total.astype(o_ref.dtype)
 
     def all_sent(ref, send):
@@ -322,12 +345,12 @@
             pltpu.VMEM((steps, half, 2 * width), bf16),
             pltpu.VMEM((steps, 2, half, width), bf16),
             pltpu.VMEM((tokens, out_width), jnp.float32),
-            pltpu.VMEM((n_col, tokens, out_width), bf16),
-            pltpu.VMEM((n_col, tokens, out_width), bf16),
+            pltpu.VMEM((n_col, 2, half, out_width), bf16),
+            pltpu.VMEM((n_col, 2, half, out_width), bf16),
             dma((2,)),
             dma((chunks,)),
             dma,
-            dma((n_col,)),
+            dma((2 * n_col,)),
             dma,
             dma((steps,)),
             dma,
@@ -335,7 +358,7 @@
             dma,
             dma((steps,)),
             dma,
-            dma((n_col,)),
+            dma((2 * n_col,)),
         ],
         compiler_params=pltpu.CompilerParams(
             collective_id=0, has_side_effects=True, vmem_limit_bytes=67043328

time: 99 us -> 96.8 us (0.978)
  Pallas kernels: 97.1 us -> 95 us
    pallas_call x1, Pallas kernels: 97.1 us -> 95 us  [on_device(): pl.pallas_call(functools.partial(body, n_row, n_col), out_shape=jax.Shape...]
where the time goes in v3:
time: 96.8 us; the launch traced here: 96.6 us
  Pallas kernels  95 us (98%)
  local copies, waits for them, and re-layouts  1.65 us (2%)
    pallas_call x1, Pallas kernels, on_device(): pl.pallas_call(functools.partial(body, n_row, n_col), out_shape=jax.Shape...  95 us

profile of v3, /device:TPU:0, one launch (start us, length us, event | category | flops | bytes accessed | tf_op | source)
XLA Modules:
  0.0 96.6 jit_solution(15458865561189269624)
XLA Ops:
  0.0 95.0 %shard_map.55 = bf16[128,896]{1,0:T(8,128)(2,1)} custom-call(s32[128,896]{1,0:T(8,128)} %codes_hbm.1, f32[14,128]{1,0:T(8,128)} %bitcast.1, bf16[896,4608]{1,0:T(8,128)(2,1)} %gate_hbm.1, bf16[896,4608]{1,0:T(8,128)(2,1)} %up_hbm.1, bf16[4608,896]{1,0:T(8,128)(2,1)} %down_hbm.1), custom_call_target="tpu_custom_call" | custom-call | tf_op jit(solution)/shard_map/pallas_call | solution.py:332
  95.0 1.6 %copy.7 = bf16[128,896]{1,0:T(8,128)(2,1)} copy(bf16[128,896]{1,0:T(8,128)(2,1)} %shard_map.55) | data formatting | bytes 458752

commit v4 on v3

--- a/solution.py
+++ b/solution.py
@@ -24,7 +24,7 @@
 def body(
     n_row, n_col, codes_hbm, scales_hbm, gate_hbm, up_hbm, down_hbm, o_ref,
     codes, scales, every, up_gate, down_w, part, from_core, from_chip, hid, acc, out_send, out_recv,
-    in_sem, w_sem, act_s, act_r, core_s, core_r, chip_s, chip_r, cross_s, cross_r, out_s, out_r,
+    in_sem, w_sem, act_s, act_r, core_s, chip_s, chip_r, cross_s, cross_r, out_s, out_r,
 ):
     _, _, half, depth = every.shape
     chunks, _, _, width = up_gate.shape
@@ -100,7 +100,7 @@
         return remote(every.at[0, side], every.at[p, side], act_s, act_r.at[at], {"col": partner(p)})
 
     def core_copy(j):
-        return remote(part.at[j, 1 - core], from_core.at[j], core_s, core_r.at[j], {"row": other_row})
+        return remote(part.at[j, 1 - core], from_core.at[j], core_s, chip_r.at[j], {"row": other_row})
 
     def chip_copy(j):
         return remote(part.at[j, core], from_chip.at[j], chip_s, chip_r.at[j], {"row": ahead_row})
@@ -173,10 +173,9 @@
         core_copy(j).start()
 
     def add_up(j):
-        core_copy(j).wait_recv()
-
         @pl.when(is_first)
         def _():
+            core_copy(j).wait_recv()
             part[j, core] = (
                 part[j, core].astype(jnp.float32) + from_core[j].astype(jnp.float32)
             ).astype(jnp.bfloat16)
@@ -184,7 +183,7 @@
 
         @pl.when(jnp.logical_not(is_first))
         def _():
-            chip_copy(j).wait_recv()
+            remote(part.at[j], part.at[j], core_s, chip_r.at[j], {"row": other_row}).wait_recv()
 
         @pl.when(jnp.logical_not(is_first) & jnp.logical_not(is_last))
         def _():
@@ -231,6 +230,16 @@
         def _():
             down_copy(c).wait()
 
+        @pl.when(k == steps - min(2, chunks))
+        def _():
+            for turn in range(1, n_col):
+                for side in range(2):
+                    out_copy(block_at(turn, side), side).wait_recv()
+            total = acc[...]
+            for p in range(1, n_col):
+                total += out_recv[p].reshape(total.shape).astype(jnp.float32)
+            acc[...] = total
+
         h = hid[j].reshape(2 * half, width)
         acc[...] += jnp.dot(h, down_w[c], preferred_element_type=jnp.float32)
 
@@ -293,16 +302,10 @@
 
     lax.fori_loop(0, down_lag + pl.cdiv(steps, PER_STEP), step, 0)
 
-    total = acc[...]
-    for turn in range(1, n_col):
-        for side in range(2):
-            out_copy(block_at(turn, side), side).wait_recv()
-    for p in range(1, n_col):
-        total += out_recv[p].reshape(total.shape).astype(jnp.float32)
-    o_ref[...] = total.astype(o_ref.dtype)
+    o_ref[...] = acc[...].astype(o_ref.dtype)
 
     def all_sent(ref, send):
-        remote(ref, ref, send, core_r.at[0], {"row": other_row}).wait_send()
+        remote(ref, ref, send, chip_r.at[0], {"row": other_row}).wait_send()
 
     all_sent(from_core, core_s)
     all_sent(hid.at[:, 0], cross_s)
@@ -352,7 +355,6 @@
             dma,
             dma((2 * n_col,)),
             dma,
-            dma((steps,)),
             dma,
             dma((steps,)),
             dma,

time: 96.8 us -> 96.3 us (level)
  no operation moved by 1% of the time
where the time goes in v4:
time: 96.3 us; the launch traced here: 96.2 us
  Pallas kernels  94.5 us (98%)
  local copies, waits for them, and re-layouts  1.65 us (2%)
    pallas_call x1, Pallas kernels, on_device(): pl.pallas_call(functools.partial(body, n_row, n_col), out_shape=jax.Shape...  94.5 us

profile of v4, /device:TPU:0, one launch (start us, length us, event | category | flops | bytes accessed | tf_op | source)
XLA Modules:
  0.0 96.2 jit_solution(14341993584355484057)
XLA Ops:
  0.0 94.5 %shard_map.55 = bf16[128,896]{1,0:T(8,128)(2,1)} custom-call(s32[128,896]{1,0:T(8,128)} %codes_hbm.1, f32[14,128]{1,0:T(8,128)} %bitcast.1, bf16[896,4608]{1,0:T(8,128)(2,1)} %gate_hbm.1, bf16[896,4608]{1,0:T(8,128)(2,1)} %up_hbm.1, bf16[4608,896]{1,0:T(8,128)(2,1)} %down_hbm.1), custom_call_target="tpu_custom_call" | custom-call | tf_op jit(solution)/shard_map/pallas_call | solution.py:335
  94.5 1.6 %copy.7 = bf16[128,896]{1,0:T(8,128)(2,1)} copy(bf16[128,896]{1,0:T(8,128)(2,1)} %shard_map.55) | data formatting | bytes 458752
